TPU v7x, 256 devices: a whole 4x4x8 slice. The times are simulated.
256 devices in a mesh: track: 4 (over y), tm: 64 (over z, x, core).
Axes of the slice: x: 4, y: 4, z: 8, core: 2. Of those that a mesh axis runs over, the one named last changes fastest.
Arguments:
- observations: float32 [8192, 16, 128], P('tm', 'track'), may hold values from -18 to 18
- dynamics: bfloat16 [256, 128, 128], P('track'), may hold values from -1 to 1
- smoother_gain: bfloat16 [256, 128, 128], P('track'), may hold values from -1 to 1
- gains: bfloat16 [256, 128], P('track'), may hold values from 0 to 1
- regime: int32 [2048], P('tm'), may hold values from 0 to 255
Outputs:
- smoothed: float32 [8192, 16, 128], P('tm', 'track')
All inputs are finite; a program needn't handle non-finite values.
Results may differ from a plain program's by a relative error of at most 0.0003.
Values may be sent and summed in bfloat16 or wider, within the bound.
A program may use at most 64 MiB of HBM per device.

v0:
```python
import functools

import jax
import jax.numpy as jnp
import numpy as np
from jax import lax
from jax.experimental import pallas as pl
from jax.experimental.pallas import tpu as pltpu
from jax.sharding import Mesh
from jax.sharding import PartitionSpec as P

TM = ("tm_0", "tm_1", "tm_2")
F32 = jnp.float32
BF16 = jnp.bfloat16
N = 128
TR = 16
ROWS = N + TR
MAP = 2 * ROWS + N
SEGS = 4
MESH = pl.DeviceIdType.MESH
VMEM = pltpu.MemorySpace.VMEM


def split2(x):
    hi = x.astype(BF16)
    return hi, (x - hi.astype(F32)).astype(BF16)


def split3(x):
    hi = x.astype(BF16)
    rest = x - hi.astype(F32)
    mid = rest.astype(BF16)
    return hi, mid, (rest - mid.astype(F32)).astype(BF16)


def dot_t(left, right):
    return lax.dot_general(left, right, (((1,), (1,)), ((), ())), preferred_element_type=F32)


def times_t(x, w):
    hi, mid, low = split3(x)
    return dot_t(jnp.concatenate([hi, mid], axis=1), jnp.concatenate([w, w], axis=1)) + dot_t(low, w)


def product(x, w):
    xh, xl = split2(x)
    wh, wl = split2(w)
    return jnp.dot(
        jnp.concatenate([xh, xl, xh], axis=1),
        jnp.concatenate([wh, wh, wl], axis=0),
        preferred_element_type=F32,
    )


PHI, V_ROW, W_MAT, W_ROW, PSI = 0, N, ROWS, ROWS + N, 2 * ROWS
AHEAD, BEHIND = (0, ROWS), (ROWS, MAP - ROWS)


def compose_ahead(left, right, out):
    both = product(left[pl.ds(0, ROWS)], right[pl.ds(PHI, N)])
    out[pl.ds(0, N)] = both[:N]
    out[pl.ds(V_ROW, TR)] = both[N:] + right[pl.ds(V_ROW, TR)]


def compose_behind(left, right, out):
    both = product(left[pl.ds(0, ROWS)], right[pl.ds(W_MAT, N)])
    last = both[N:] + right[pl.ds(W_ROW, TR)]
    back = product(jnp.concatenate([both[:N], last, right[pl.ds(PSI, N)]], axis=0), left[pl.ds(PSI, N)])
    out[pl.ds(W_MAT, ROWS)] = back[:ROWS] + left[pl.ds(W_MAT, ROWS)]
    out[pl.ds(PSI, N)] = back[ROWS:]


def middle_x(x, left):
    return product(x, left[pl.ds(PHI, N)]) + left[pl.ds(V_ROW, TR)]


def middle_u(x_mid, u, right):
    mats = jnp.concatenate([right[pl.ds(W_MAT, N)], right[pl.ds(PSI, N)]], axis=0)
    return product(jnp.concatenate([x_mid, u], axis=1), mats) + right[pl.ds(W_ROW, TR)]


def tree_of(leaves, nodes):
    levels, used = [leaves], 0
    while len(levels[-1]) > 1:
        row = [nodes.at[used + i] for i in range(len(levels[-1]) // 2)]
        used += len(row)
        levels.append(row)
    return levels


def fill(levels, compose):
    for below, row in zip(levels, levels[1:]):
        for i, node in enumerate(row):
            compose(below[2 * i], below[2 * i + 1], node)


def descend(x, u, levels, position):
    for level in range(len(levels) - 2, -1, -1):
        row = levels[level]
        bit = lax.rem(lax.div(position, 2**level), 2)
        above = lax.div(position, 2 ** (level + 1))
        best_x, best_u = None, None
        for i in range(len(row) // 2):
            x_mid = middle_x(x, row[2 * i])
            u_mid = middle_u(x_mid, u, row[2 * i + 1])
            best_x = x_mid if best_x is None else jnp.where(above == i, x_mid, best_x)
            best_u = u_mid if best_u is None else jnp.where(above == i, u_mid, best_u)
        x = jnp.where(bit == 1, best_x, x)
        u = jnp.where(bit == 1, u, best_u)
    return x, u


class Wires:
    def __init__(self, send, recv):
        self.send, self.recv, self.used = send, recv, 0
        self.pending = []

    def make(self, src, dst, **peer):
        copy = pltpu.make_async_remote_copy(
            src_ref=src,
            dst_ref=dst,
            send_sem=self.send.at[self.used],
            recv_sem=self.recv.at[self.used],
            device_id=peer,
            device_id_type=MESH,
        )
        self.used += 1
        return copy

    def go(self, src, dst, **peer):
        copy = self.make(src, dst, **peer)
        copy.start()
        self.pending.append(copy)
        return copy

    def close(self):
        for copy in self.pending:
            copy.wait_send()


def compose_psi(left, right, out):
    out[pl.ds(PSI, N)] = product(right[pl.ds(PSI, N)], left[pl.ds(PSI, N)])


def compose_w(left, right, out):
    both = product(left[pl.ds(0, ROWS)], right[pl.ds(W_MAT, N)])
    last = both[N:] + right[pl.ds(W_ROW, TR)]
    back = product(jnp.concatenate([both[:N], last], axis=0), left[pl.ds(PSI, N)])
    out[pl.ds(W_MAT, ROWS)] = back + left[pl.ds(W_MAT, ROWS)]


class Ring:
    def __init__(self, wires, buf, axis, size, first, count):
        self.wires, self.buf, self.axis, self.size = wires, buf, axis, size
        self.me = lax.axis_index(axis)
        half = -(-count // 16) * 8
        self.rows = [pl.ds(first, count)]
        if size > 2:
            self.rows = [
                pl.ds(pl.multiple_of(first, 8), half),
                pl.ds(pl.multiple_of(first + half, 8), count - half),
            ]

    def send(self, who, part, there):
        piece = self.buf.at[who, self.rows[part]]
        return self.wires.go(piece, piece, **{self.axis: there})

    def start(self):
        if self.size == 2:
            self.rest = [self.send(self.me, 0, 1 - self.me)]
        if self.size > 2:
            self.right = lax.rem(self.me + 1, self.size)
            self.left = lax.rem(self.me + self.size - 1, self.size)
            self.first = [self.send(self.me, 0, self.right), self.send(self.me, 1, self.left)]
            self.rest = [self.send(self.me, 1, self.right), self.send(self.me, 0, self.left)]

    def relay(self):
        if self.size > 2:
            self.first[0].wait_recv()
            self.rest.append(self.send(self.left, 0, self.right))
            self.first[1].wait_recv()
            self.rest.append(self.send(self.right, 1, self.left))

    def finish(self):
        if self.size > 1:
            for copy in self.rest:
                copy.wait_recv()


class Merge:
    def __init__(self, wires, cand, relay, arrived, y):
        self.wires, self.cand, self.relay_buf, self.arrived, self.y = wires, cand, relay, arrived, y
        self.right, self.left, self.far = (lax.rem(y + k, 4) for k in (1, 3, 2))
        self.each = cand.shape[0] // 4
        self.half = self.each // 2

    def part(self, owner, side):
        return pl.ds(owner * self.each + side * self.half, self.half)

    def start(self):
        go, cand, half = self.wires.go, self.cand, self.half
        low, high = pl.ds(0, half), pl.ds(half, half)
        self.via = [
            go(cand.at[self.part(self.far, 0)], self.relay_buf.at[0], track=self.right),
            go(cand.at[self.part(self.far, 1)], self.relay_buf.at[1], track=self.left),
        ]
        self.rest = [
            go(cand.at[self.part(self.right, 1)], self.arrived.at[0, high], track=self.right),
            go(cand.at[self.part(self.left, 0)], self.arrived.at[1, low], track=self.left),
        ]

    def relay(self):
        go, half = self.wires.go, self.half
        for side, (there, rows) in enumerate(((self.right, pl.ds(0, half)), (self.left, pl.ds(half, half)))):
            self.via[side].wait_recv()
            self.relay_buf[2 + side] = self.relay_buf[side] + self.cand[self.part(there, side)]
            self.rest.append(go(self.relay_buf.at[2 + side], self.arrived.at[side, rows], track=there))

    def finish(self, out):
        for copy in self.rest:
            copy.wait_recv()
        out[...] = self.cand[pl.ds(self.y * self.each, self.each)] + (self.arrived[0] + self.arrived[1])


def forward_pass(a_own, k_own, o_all, x_all, e_all):
    count = a_own.shape[0]
    dwell = o_all.shape[0] // count
    per = count // SEGS
    eye = (
        lax.broadcasted_iota(jnp.int32, (N, N), 0) == lax.broadcasted_iota(jnp.int32, (N, N), 1)
    ).astype(F32)
    start = jnp.concatenate([eye, jnp.zeros((TR, N), F32)], axis=0)
    blank = jnp.zeros((N, N), F32)

    def some(i, xs):
        new_x = list(xs)
        for step in range(dwell):
            for seg in range(SEGS):
                block = seg * per + i
                t = block * dwell + step
                pred = times_t(new_x[seg], a_own[block])
                obs = jnp.concatenate([blank, o_all[t]], axis=0)
                e = k_own[pl.ds(block, 1)] * (obs - pred)
                e_all[t] = e
                x_all[t] = pred + e
                new_x[seg] = pred + e
        return tuple(new_x)

    return lax.fori_loop(0, per, some, (start,) * SEGS)


def backward_pass(g_own, x_all, e_all, hi_ref, lo_ref, s_all):
    count = g_own.shape[0]
    dwell = x_all.shape[0] // count
    per = count // SEGS
    eye = (
        lax.broadcasted_iota(jnp.int32, (N, N), 0) == lax.broadcasted_iota(jnp.int32, (N, N), 1)
    ).astype(F32)

    def keep(t, row, value):
        hi, low = split2(value)
        hi_ref[t, pl.ds(row, N)] = hi
        lo_ref[t, pl.ds(row, N)] = low

    def some(i, carry):
        new_u, new_p = list(carry[0]), list(carry[1])
        for step in range(dwell):
            for seg in range(SEGS):
                block = seg * per + per - 1 - i
                t = block * dwell + dwell - 1 - step
                s = x_all[t] + new_u[seg]
                keep(t, 0, s[:N])
                keep(t, N, new_p[seg])
                s_all[t] = s[N:]
                back = times_t(jnp.concatenate([new_u[seg] + e_all[t], new_p[seg]], axis=0), g_own[block])
                new_u[seg], new_p[seg] = back[:ROWS], back[ROWS:]
        return tuple(new_u), tuple(new_p)

    return lax.fori_loop(0, per, some, ((jnp.zeros((ROWS, N), F32),) * SEGS, (eye,) * SEGS))


def final_pass(x, u, levels, hi_ref, lo_ref, s_all, out_buf, sent):
    spans = [(x, u)]
    for row in levels[-2::-1]:
        new = []
        for i, (x, u) in enumerate(spans):
            x_mid = middle_x(x, row[2 * i])
            new += [(x, middle_u(x_mid, u, row[2 * i + 1])), (x_mid, u)]
        spans = new
    per = s_all.shape[0] // SEGS
    four = TR // 4
    for seg, (x, u) in enumerate(spans):
        hi, low = split2(jnp.concatenate([x, u], axis=1))
        both = jnp.concatenate([hi, low], axis=0)
        for pair in range(per // 2):
            outs = []
            for t in (seg * per + 2 * pair, seg * per + 2 * pair + 1):
                first = jnp.dot(both, hi_ref[t], preferred_element_type=F32)
                second = jnp.dot(hi, lo_ref[t], preferred_element_type=F32)
                outs.append(s_all[t] + ((first[:TR] + first[TR:]) + second))
            for group in range(4):
                rows = slice(four * group, four * group + four)
                out_buf[group, pl.ds((seg * per + 2 * pair) * four, 2 * four)] = jnp.concatenate(
                    [outs[0][rows], outs[1][rows]], axis=0
                )
        sent(seg * per * four, per * four)


def main_kernel(sizes, *refs):
    (ids, dyn, smooth, gain, obs_in, out_ref, tab_a, tab_g, tab_s, tab_k, ca, cg, ck, local, relay, arrived, k_buf, o_buf, o_way, a_own, g_own, k_own, o_all, x_all, e_all,
     hi_ref, lo_ref, s_all, segs, segnode, ybuf, ynode, cbuf, cnode, xbuf, xnode, zpv, zps, zc, out_buf,
     send, recv) = refs
    ny, nz, nx, nc = sizes
    y, z, x, c = (lax.axis_index(a) for a in ("track",) + TM)
    each = obs_in.shape[0] // 4
    blocks = a_own.shape[0]
    own_rows = pl.ds(pl.multiple_of(y * each, each), each)
    fetch_a = pltpu.make_async_copy(dyn, tab_a, local.at[0])
    fetch_g = pltpu.make_async_copy(smooth, tab_g, local.at[1])
    fetch_o = pltpu.make_async_copy(obs_in.at[own_rows], o_buf.at[y], local.at[2])
    fetch_k = pltpu.make_async_copy(gain, tab_s, local.at[3])
    for copy in (fetch_k, fetch_a, fetch_g, fetch_o):
        copy.start()
    barrier = pltpu.get_barrier_semaphore()
    peers = []
    for axis, me, size in (("track", y, ny), ("tm_0", z, nz), ("tm_1", x, nx), ("tm_2", c, nc)):
        for step in range(1, size):
            peers.append({axis: lax.rem(me + step, size)})
    for peer in peers:
        pl.semaphore_signal(barrier, inc=1, device_id=peer, device_id_type=MESH)
    fetch_k.wait()
    tab_k[...] = tab_s[...].astype(F32)
    owned = tab_a.shape[0]
    zero_mat = jnp.zeros((N, N), BF16)

    def picked(b):
        row = ids[b] - y * owned
        return jnp.logical_and(row >= 0, row < owned), jnp.clip(row, 0, owned - 1)

    def pick_a(b, _):
        here, row = picked(b)
        ca[b] = jnp.where(here, tab_a[row], zero_mat)
        ck[pl.ds(b, 1)] = jnp.where(here, tab_k[pl.ds(row, 1)], 0.0)
        return 0

    def pick_g(b, _):
        here, row = picked(b)
        cg[b] = jnp.where(here, tab_g[row], zero_mat)
        return 0

    fetch_a.wait()
    lax.fori_loop(0, ca.shape[0], pick_a, 0)
    pl.semaphore_wait(barrier, len(peers))
    wires = Wires(send, recv)
    right, left, far = others = [lax.rem(y + k, 4) for k in (1, 3, 2)]

    a_move = Merge(wires, ca, relay.at[0], arrived.at[0], y)
    g_move = Merge(wires, cg, relay.at[1], arrived.at[1], y)
    a_move.start()
    small = []
    half = each // 2

    def obs_rows(owner, first, count):
        return obs_in.at[pl.ds(pl.multiple_of(owner * each + first, 8), count)]

    for there in (right, left):
        small.append(wires.go(obs_rows(there, 0, each), o_buf.at[y], track=there))
    small.append(wires.go(obs_rows(far, 0, half), o_buf.at[y, pl.ds(0, half)], track=far))
    detour = wires.go(obs_rows(far, half, half), o_way.at[0], track=left)
    for there in others:
        small.append(wires.go(ck.at[pl.ds(pl.multiple_of(there * blocks, blocks), blocks)], k_buf.at[y], track=there))
    k_buf[y] = ck[pl.ds(pl.multiple_of(y * blocks, blocks), blocks)]
    fetch_g.wait()
    lax.fori_loop(0, cg.shape[0], pick_g, 0)
    a_move.relay()
    detour.wait_recv()
    small.append(wires.go(o_way.at[0], o_buf.at[right, pl.ds(half, half)], track=left))
    g_move.start()
    a_move.finish(a_own)
    for copy in small:
        copy.wait_recv()
    fetch_o.wait()
    k_own[...] = (k_buf[0] + k_buf[1]) + (k_buf[2] + k_buf[3])
    four = TR // 4

    def in_steps(p, _):
        tiles = [o_buf[s, pl.ds(pl.multiple_of(p * 2 * four, 8), 2 * four)] for s in range(4)]
        o_all[2 * p] = jnp.concatenate([tile[:four] for tile in tiles], axis=0)
        o_all[2 * p + 1] = jnp.concatenate([tile[four:] for tile in tiles], axis=0)
        return 0

    lax.fori_loop(0, each // (2 * four), in_steps, 0)

    xs = forward_pass(a_own, k_own, o_all, x_all, e_all)
    for seg in range(SEGS):
        segs[seg, pl.ds(0, ROWS)] = xs[seg]
    stree = tree_of([segs.at[i] for i in range(SEGS)], segnode)
    ytree = tree_of([ybuf.at[i] for i in range(ny)], ynode)
    ctree = tree_of([cbuf.at[i] for i in range(nc)], cnode)
    xtree = tree_of([xbuf.at[i] for i in range(nx)], xnode)
    share_a, share_b = AHEAD[1] // nc, BEHIND[1] // nc
    own_a, own_b = c * share_a, BEHIND[0] + c * share_b
    y_ahead = Ring(wires, ybuf, "track", ny, *AHEAD)
    y_behind = Ring(wires, ybuf, "track", ny, *BEHIND)
    c_ahead = Ring(wires, cbuf, "tm_2", nc, *AHEAD)
    c_behind = Ring(wires, cbuf, "tm_2", nc, *BEHIND)
    x_ahead = Ring(wires, xbuf, "tm_1", nx, own_a, share_a)
    x_behind = Ring(wires, xbuf, "tm_1", nx, own_b, share_b)
    fill(stree, compose_ahead)
    ybuf[y, pl.ds(0, ROWS)] = stree[-1][0][pl.ds(0, ROWS)]
    g_move.relay()
    y_ahead.start()
    g_move.finish(g_own)
    y_ahead.relay()

    us, ps = backward_pass(g_own, x_all, e_all, hi_ref, lo_ref, s_all)
    for seg in range(SEGS):
        segs[seg, pl.ds(W_MAT, ROWS)] = us[seg]
        segs[seg, pl.ds(PSI, N)] = ps[seg]
    fill(stree, compose_behind)
    ybuf[y, pl.ds(W_MAT, ROWS + N)] = stree[-1][0][pl.ds(W_MAT, ROWS + N)]
    y_behind.start()

    def share_start(own, share):
        rows = pl.ds(pl.multiple_of(own, 8), share)
        parts = [xbuf.at[lax.rem(x + step, nx), rows] for step in range(1, nx)] if nc > 1 else []
        return [wires.go(part, part, tm_2=1 - c) for part in parts]

    def to_slabs(buf, rows, later):
        mine = pl.ds(pl.multiple_of(c * (rows // nc), 8), rows // nc)
        part = buf.at[z, mine]
        moves = []
        for step in range(1, nz):
            there = z + step if later else z - step
            copy = wires.make(part, part, tm_0=jnp.clip(there, 0, nz - 1))
            use = there < nz if later else there >= 0
            moves.append((copy, use))
            pl.when(use)(copy.start)
        return mine, moves

    def from_slabs(buf, mine, moves, later):
        shared = []
        for step, (copy, _) in enumerate(moves, 1):
            source = z - step if later else z + step
            use = source >= 0 if later else source < nz
            pl.when(use)(copy.wait_recv)
            if nc > 1:
                part = buf.at[jnp.clip(source, 0, nz - 1), mine]
                over = wires.make(part, part, tm_2=1 - c)
                pl.when(use)(over.start)
                shared.append((over, use))
        for copy, use in shared:
            pl.when(use)(copy.wait_recv)
        for copy, use in moves + shared:
            pl.when(use)(copy.wait_send)

    y_ahead.finish()
    fill(ytree, compose_ahead)
    cbuf[c, pl.ds(0, ROWS)] = ytree[-1][0][pl.ds(0, ROWS)]
    c_ahead.start()
    c_ahead.finish()
    fill(ctree, compose_ahead)
    xbuf[x, pl.ds(0, ROWS)] = ctree[-1][0][pl.ds(0, ROWS)]
    x_ahead.start()
    y_behind.relay()
    x_ahead.relay()
    y_behind.finish()
    fill(ytree, compose_behind)
    cbuf[c, pl.ds(W_MAT, ROWS + N)] = ytree[-1][0][pl.ds(W_MAT, ROWS + N)]
    c_behind.start()
    x_ahead.finish()
    shared = share_start(own_a, share_a)
    c_behind.finish()
    fill(ctree, compose_behind)
    xbuf[x, pl.ds(W_MAT, ROWS + N)] = ctree[-1][0][pl.ds(W_MAT, ROWS + N)]
    x_behind.start()
    for copy in shared:
        copy.wait_recv()
    fill(xtree, compose_ahead)
    total = xtree[-1][0]
    zpv[z] = total[pl.ds(0, ROWS)]
    z_ahead = to_slabs(zpv, ROWS, True)
    x_behind.relay()
    x_behind.finish()
    for copy in share_start(own_b, share_b):
        copy.wait_recv()
    fill(xtree, compose_psi)
    zps[z] = total[pl.ds(PSI, N)]
    z_behind = to_slabs(zps, N, False)
    fill(xtree, compose_w)
    from_slabs(zpv, *z_ahead, True)

    zero = jnp.zeros((TR, N), F32)
    entering, state = zero, zero
    for i in range(nz - 1):
        got = jnp.minimum(i, z)
        after = zpv[got, pl.ds(V_ROW, TR)]
        if i > 0:
            after = after + product(state, zpv[got, pl.ds(PHI, N)])
        state = after
        entering = jnp.where(z == i + 1, state, entering)
    zc[z] = product(entering, total[pl.ds(W_MAT, N)]) + total[pl.ds(W_ROW, TR)]
    part = zc.at[z]
    group = [wires.go(part, part, tm_0=lax.rem(z + step, nz)) for step in range(1, nz)]
    from_slabs(zps, *z_behind, False)
    for copy in group:
        copy.wait_recv()
    leaving, state = zero, zero
    for i in range(nz - 1, 0, -1):
        after = zc[i]
        if i < nz - 1:
            after = after + product(state, zps[jnp.maximum(i, z)])
        state = after
        leaving = jnp.where(z == i - 1, state, leaving)

    xv, uv = descend(entering, leaving, xtree, x)
    xv, uv = descend(xv, uv, ctree, c)
    xv, uv = descend(xv, uv, ytree, y)

    homes, detours = [], []

    def target(first, count):
        return out_ref.at[pl.ds(pl.multiple_of(y * each + first, 8), count)]

    def sent(first, count):
        rows = pl.ds(first, count)
        if first < half:
            detours.append((wires.go(out_buf.at[far, rows], o_way.at[1, rows], track=left), rows, first, count))
        for there in (right, left) if first < half else others:
            homes.append(wires.go(out_buf.at[there, rows], target(first, count), track=there))

    final_pass(xv, uv, stree, hi_ref, lo_ref, s_all, out_buf, sent)
    out_ref[own_rows] = out_buf[y]
    for copy, rows, first, count in detours:
        copy.wait_recv()
        there = out_ref.at[pl.ds(pl.multiple_of(right * each + first, 8), count)]
        homes.append(wires.go(o_way.at[1, rows], there, track=left))
    for copy in homes:
        copy.wait_recv()
    wires.close()


def main_call(sizes, ids, dyn, smooth, gain, obs):
    ny, nz, nx, nc = sizes
    count, owned = ids.shape[0], dyn.shape[0]
    blocks = count // ny
    each = obs.shape[0] // ny
    steps = each // (TR // ny)
    links = 20 + 30 + 2 * (1 + nx) + 5 * nz + 3 * SEGS
    hbm = pl.BlockSpec(memory_space=pltpu.MemorySpace.HBM)
    vmem = pl.BlockSpec(memory_space=VMEM)
    return pl.pallas_call(
        functools.partial(main_kernel, sizes),
        out_shape=jax.ShapeDtypeStruct(obs.shape, F32),
        in_specs=[pl.BlockSpec(memory_space=pltpu.MemorySpace.SMEM), hbm, hbm, hbm, hbm],
        out_specs=vmem,
        scratch_shapes=[
            pltpu.VMEM((owned, N, N), BF16),
            pltpu.VMEM((owned, N, N), BF16),
            pltpu.VMEM((owned, N), BF16),
            pltpu.VMEM((owned, N), F32),
            pltpu.VMEM((count, N, N), BF16),
            pltpu.VMEM((count, N, N), BF16),
            pltpu.VMEM((count, N), F32),
            pltpu.SemaphoreType.DMA((4,)),
            pltpu.VMEM((2, 4, blocks // 2, N, N), BF16),
            pltpu.VMEM((2, 2, blocks, N, N), BF16),
            pltpu.VMEM((4, blocks, N), F32),
            pltpu.VMEM((4, each, N), F32),
            pltpu.VMEM((2, each // 2, N), F32),
            pltpu.VMEM((blocks, N, N), BF16),
            pltpu.VMEM((blocks, N, N), BF16),
            pltpu.VMEM((blocks, N), F32),
            pltpu.VMEM((steps, TR, N), F32),
            pltpu.VMEM((steps, ROWS, N), F32),
            pltpu.VMEM((steps, ROWS, N), F32),
            pltpu.VMEM((steps, 2 * N, N), BF16),
            pltpu.VMEM((steps, 2 * N, N), BF16),
            pltpu.VMEM((steps, TR, N), F32),
            pltpu.VMEM((SEGS, MAP, N), F32),
            pltpu.VMEM((SEGS - 1, MAP, N), F32),
            pltpu.VMEM((ny, MAP, N), F32),
            pltpu.VMEM((max(ny - 1, 1), MAP, N), F32),
            pltpu.VMEM((nc, MAP, N), F32),
            pltpu.VMEM((max(nc - 1, 1), MAP, N), F32),
            pltpu.VMEM((nx, MAP, N), F32),
            pltpu.VMEM((max(nx - 1, 1), MAP, N), F32),
            pltpu.VMEM((nz, ROWS, N), F32),
            pltpu.VMEM((nz, N, N), F32),
            pltpu.VMEM((nz, TR, N), F32),
            pltpu.VMEM((4, each, N), F32),
            pltpu.SemaphoreType.DMA((links,)),
            pltpu.SemaphoreType.DMA((links,)),
        ],
        compiler_params=pltpu.CompilerParams(
            collective_id=1, has_side_effects=True, vmem_limit_bytes=67043328
        ),
        name="smooth",
    )(ids, dyn, smooth, gain, obs)


def body(sizes, observations, dynamics, smoother_gain, gains, regime):
    out = main_call(sizes, regime, dynamics, smoother_gain, gains, observations.reshape(-1, N))
    return out.reshape(observations.shape)


def build(torus):
    sizes = tuple(torus.shape[a] for a in ("track",) + TM)
    placed = (
        P(TM, "track", None),
        P("track", None, None),
        P("track", None, None),
        P("track", None),
        P(TM),
    )
    return jax.shard_map(
        functools.partial(body, sizes),
        mesh=torus,
        in_specs=placed,
        out_specs=P(TM, "track", None),
        check_vma=False,
    )


def solution(mesh):
    return build(Mesh(mesh.devices.reshape(mesh.shape["track"], 8, 4, 2), ("track",) + TM))
```

profile of v0, /device:TPU:40, one launch (start us, length us, event | category | flops | bytes accessed | tf_op | source)
XLA Modules:
  0.0 77.4 jit_solution(17642789866307648260)
XLA Ops:
  0.0 75.7 %smooth.1 = f32[512,128]{1,0:T(8,128)} custom-call(s32[32]{0:T(128)} %refs_0_.1, bf16[64,128,128]{2,1,0:T(8,128)(2,1)} %refs_1_.1, bf16[64,128,128]{2,1,0:T(8,128)(2,1)} %refs_2_.1, bf16[64,128]{1,0:T(8,128)(2,1)} %refs_3_.1, f32[512,128]{1,0:T(8,128)} %bitcast.3), custom_call_target="tpu_custom_call" | custom-call | tf_op jit(solution)/shard_map/smooth/pallas_call | solution.py:552
  75.7 1.7 %copy.7 = f32[128,4,128]{2,1,0:T(4,128)} copy(f32[128,4,128]{2,1,0:T(4,128)} %bitcast.2) | data formatting | bytes 524288
where the time goes:
time: 77.5 us; the launch traced here: 77.4 us
  Pallas kernels  75.7 us (98%)
  local copies, waits for them, and re-layouts  1.67 us (2%)
    pallas_call x1, Pallas kernels, main_call(): pl.pallas_call(functools.partial(main_kernel, sizes), out_shape=jax.Shape...  75.7 us
    unnamed x1, local copies, waits for them, and re-layouts  1.67 us

commit v1 on v0

--- a/solution.py
+++ b/solution.py
@@ -140,13 +140,6 @@
 
 def compose_psi(left, right, out):
     out[pl.ds(PSI, N)] = product(right[pl.ds(PSI, N)], left[pl.ds(PSI, N)])
-
-
-def compose_w(left, right, out):
-    both = product(left[pl.ds(0, ROWS)], right[pl.ds(W_MAT, N)])
-    last = both[N:] + right[pl.ds(W_ROW, TR)]
-    back = product(jnp.concatenate([both[:N], last], axis=0), left[pl.ds(PSI, N)])
-    out[pl.ds(W_MAT, ROWS)] = back + left[pl.ds(W_MAT, ROWS)]
 
 
 class Ring:
@@ -433,7 +426,7 @@
         for step in range(1, nz):
             there = z + step if later else z - step
             copy = wires.make(part, part, tm_0=jnp.clip(there, 0, nz - 1))
-            use = there < nz if later else there >= 0
+            use = there < nz if later else jnp.logical_and(there >= 0, z < nz - 1)
             moves.append((copy, use))
             pl.when(use)(copy.start)
         return mine, moves
@@ -442,7 +435,7 @@
         shared = []
         for step, (copy, _) in enumerate(moves, 1):
             source = z - step if later else z + step
-            use = source >= 0 if later else source < nz
+            use = source >= 0 if later else source < nz - 1
             pl.when(use)(copy.wait_recv)
             if nc > 1:
                 part = buf.at[jnp.clip(source, 0, nz - 1), mine]
@@ -487,7 +480,6 @@
     fill(xtree, compose_psi)
     zps[z] = total[pl.ds(PSI, N)]
     z_behind = to_slabs(zps, N, False)
-    fill(xtree, compose_w)
     from_slabs(zpv, *z_ahead, True)
 
     zero = jnp.zeros((TR, N), F32)
@@ -499,7 +491,18 @@
             after = after + product(state, zpv[got, pl.ds(PHI, N)])
         state = after
         entering = jnp.where(z == i + 1, state, entering)
-    zc[z] = product(entering, total[pl.ds(W_MAT, N)]) + total[pl.ds(W_ROW, TR)]
+    chip_x = [entering]
+    for i in range(nx - 1):
+        chip_x.append(middle_x(chip_x[-1], xbuf.at[i]))
+    chip_w = [product(chip_x[i], xbuf[i, pl.ds(W_MAT, N)]) + xbuf[i, pl.ds(W_ROW, TR)] for i in range(nx)]
+
+    def leave_chips(state):
+        states = [state]
+        for i in range(nx - 1, -1, -1):
+            states.append(chip_w[i] if states[-1] is None else product(states[-1], xbuf[i, pl.ds(PSI, N)]) + chip_w[i])
+        return states[::-1]
+
+    zc[z] = leave_chips(None)[0]
     part = zc.at[z]
     group = [wires.go(part, part, tm_0=lax.rem(z + step, nz)) for step in range(1, nz)]
     from_slabs(zps, *z_behind, False)
@@ -513,7 +516,10 @@
         state = after
         leaving = jnp.where(z == i - 1, state, leaving)
 
-    xv, uv = descend(entering, leaving, xtree, x)
+    chip_u = leave_chips(leaving)
+    xv, uv = chip_x[0], chip_u[1]
+    for i in range(1, nx):
+        xv, uv = jnp.where(x == i, chip_x[i], xv), jnp.where(x == i, chip_u[i + 1], uv)
     xv, uv = descend(xv, uv, ctree, c)
     xv, uv = descend(xv, uv, ytree, y)
 

time: 77.5 us -> 77.4 us (level); the launches traced: 77.4 us -> 76.3 us
  Pallas kernels: 75.7 us -> 74.6 us
    pallas_call x1, Pallas kernels: 75.7 us -> 74.6 us  [main_call(): pl.pallas_call(functools.partial(main_kernel, sizes), out_shape=jax.Shape...]
where the time goes in v1:
time: 77.4 us; the launch traced here: 76.3 us
  Pallas kernels  74.6 us (96%)
  local copies, waits for them, and re-layouts  1.67 us (2%)
    pallas_call x1, Pallas kernels, main_call(): pl.pallas_call(functools.partial(main_kernel, sizes), out_shape=jax.Shape...  74.6 us
    unnamed x1, local copies, waits for them, and re-layouts  1.67 us

profile of v1, /device:TPU:40, one launch (start us, length us, event | category | flops | bytes accessed | tf_op | source)
XLA Modules:
  0.0 76.3 jit_solution(3591034210986590166)
XLA Ops:
  0.0 74.6 %smooth.1 = f32[512,128]{1,0:T(8,128)} custom-call(s32[32]{0:T(128)} %refs_0_.1, bf16[64,128,128]{2,1,0:T(8,128)(2,1)} %refs_1_.1, bf16[64,128,128]{2,1,0:T(8,128)(2,1)} %refs_2_.1, bf16[64,128]{1,0:T(8,128)(2,1)} %refs_3_.1, f32[512,128]{1,0:T(8,128)} %bitcast.3), custom_call_target="tpu_custom_call" | custom-call | tf_op jit(solution)/shard_map/smooth/pallas_call | solution.py:558
  74.6 1.7 %copy.7 = f32[128,4,128]{2,1,0:T(4,128)} copy(f32[128,4,128]{2,1,0:T(4,128)} %bitcast.2) | data formatting | bytes 524288

commit v2 on v1

--- a/solution.py
+++ b/solution.py
@@ -74,11 +74,6 @@
     return product(x, left[pl.ds(PHI, N)]) + left[pl.ds(V_ROW, TR)]
 
 
-def middle_u(x_mid, u, right):
-    mats = jnp.concatenate([right[pl.ds(W_MAT, N)], right[pl.ds(PSI, N)]], axis=0)
-    return product(jnp.concatenate([x_mid, u], axis=1), mats) + right[pl.ds(W_ROW, TR)]
-
-
 def tree_of(leaves, nodes):
     levels, used = [leaves], 0
     while len(levels[-1]) > 1:
@@ -94,20 +89,34 @@
             compose(below[2 * i], below[2 * i + 1], node)
 
 
-def descend(x, u, levels, position):
+def cross(x_mid, right):
+    return product(x_mid, right[pl.ds(W_MAT, N)]) + right[pl.ds(W_ROW, TR)]
+
+
+def descend_x(x, levels, position):
+    plan = []
     for level in range(len(levels) - 2, -1, -1):
         row = levels[level]
         bit = lax.rem(lax.div(position, 2**level), 2)
         above = lax.div(position, 2 ** (level + 1))
-        best_x, best_u = None, None
+        best, terms = None, []
         for i in range(len(row) // 2):
             x_mid = middle_x(x, row[2 * i])
-            u_mid = middle_u(x_mid, u, row[2 * i + 1])
-            best_x = x_mid if best_x is None else jnp.where(above == i, x_mid, best_x)
-            best_u = u_mid if best_u is None else jnp.where(above == i, u_mid, best_u)
-        x = jnp.where(bit == 1, best_x, x)
-        u = jnp.where(bit == 1, u, best_u)
-    return x, u
+            terms.append((row[2 * i + 1], cross(x_mid, row[2 * i + 1])))
+            best = x_mid if best is None else jnp.where(above == i, x_mid, best)
+        plan.append((bit, above, terms))
+        x = jnp.where(bit == 1, best, x)
+    return x, plan
+
+
+def descend_u(u, plan):
+    for bit, above, terms in plan:
+        best = None
+        for i, (right, term) in enumerate(terms):
+            u_mid = product(u, right[pl.ds(PSI, N)]) + term
+            best = u_mid if best is None else jnp.where(above == i, u_mid, best)
+        u = jnp.where(bit == 1, u, best)
+    return u
 
 
 class Wires:
@@ -242,7 +251,7 @@
     return lax.fori_loop(0, per, some, (start,) * SEGS)
 
 
-def backward_pass(g_own, x_all, e_all, hi_ref, lo_ref, s_all):
+def backward_pass(g_own, x_all, e_all, hi_ref, lo_ref, s_all, between):
     count = g_own.shape[0]
     dwell = x_all.shape[0] // count
     per = count // SEGS
@@ -269,31 +278,50 @@
                 new_u[seg], new_p[seg] = back[:ROWS], back[ROWS:]
         return tuple(new_u), tuple(new_p)
 
-    return lax.fori_loop(0, per, some, ((jnp.zeros((ROWS, N), F32),) * SEGS, (eye,) * SEGS))
-
-
-def final_pass(x, u, levels, hi_ref, lo_ref, s_all, out_buf, sent):
-    spans = [(x, u)]
+    carry = lax.fori_loop(0, per // 2, some, ((jnp.zeros((ROWS, N), F32),) * SEGS, (eye,) * SEGS))
+    between()
+    return lax.fori_loop(per // 2, per, some, carry)
+
+
+def response(state, hi_ref, lo_ref, t, row):
+    hi, low = split2(state)
+    first = jnp.dot(jnp.concatenate([hi, low], axis=0), hi_ref[t, pl.ds(row, N)], preferred_element_type=F32)
+    return (first[:TR] + first[TR:]) + jnp.dot(hi, lo_ref[t, pl.ds(row, N)], preferred_element_type=F32)
+
+
+def final_x(x, levels, hi_ref, lo_ref, s_all):
+    xs, plan = [x], []
     for row in levels[-2::-1]:
+        new, terms = [], []
+        for i, x in enumerate(xs):
+            x_mid = middle_x(x, row[2 * i])
+            new += [x, x_mid]
+            terms.append((row[2 * i + 1], cross(x_mid, row[2 * i + 1])))
+        xs = new
+        plan.append(terms)
+    per = s_all.shape[0] // SEGS
+    for seg, x in enumerate(xs):
+        for t in range(seg * per, seg * per + per):
+            s_all[t] = s_all[t] + response(x, hi_ref, lo_ref, t, 0)
+    return plan
+
+
+def final_u(u, plan, hi_ref, lo_ref, s_all, out_buf, sent):
+    us = [u]
+    for terms in plan:
         new = []
-        for i, (x, u) in enumerate(spans):
-            x_mid = middle_x(x, row[2 * i])
-            new += [(x, middle_u(x_mid, u, row[2 * i + 1])), (x_mid, u)]
-        spans = new
+        for u, (right, term) in zip(us, terms):
+            new += [product(u, right[pl.ds(PSI, N)]) + term, u]
+        us = new
     per = s_all.shape[0] // SEGS
     four = TR // 4
-    for seg, (x, u) in enumerate(spans):
-        hi, low = split2(jnp.concatenate([x, u], axis=1))
-        both = jnp.concatenate([hi, low], axis=0)
+    for seg, u in enumerate(us):
         for pair in range(per // 2):
-            outs = []
-            for t in (seg * per + 2 * pair, seg * per + 2 * pair + 1):
-                first = jnp.dot(both, hi_ref[t], preferred_element_type=F32)
-                second = jnp.dot(hi, lo_ref[t], preferred_element_type=F32)
-                outs.append(s_all[t] + ((first[:TR] + first[TR:]) + second))
+            first = seg * per + 2 * pair
+            outs = [s_all[t] + response(u, hi_ref, lo_ref, t, N) for t in (first, first + 1)]
             for group in range(4):
                 rows = slice(four * group, four * group + four)
-                out_buf[group, pl.ds((seg * per + 2 * pair) * four, 2 * four)] = jnp.concatenate(
+                out_buf[group, pl.ds(first * four, 2 * four)] = jnp.concatenate(
                     [outs[0][rows], outs[1][rows]], axis=0
                 )
         sent(seg * per * four, per * four)
@@ -404,9 +432,8 @@
     g_move.relay()
     y_ahead.start()
     g_move.finish(g_own)
-    y_ahead.relay()
-
-    us, ps = backward_pass(g_own, x_all, e_all, hi_ref, lo_ref, s_all)
+
+    us, ps = backward_pass(g_own, x_all, e_all, hi_ref, lo_ref, s_all, y_ahead.relay)
     for seg in range(SEGS):
         segs[seg, pl.ds(W_MAT, ROWS)] = us[seg]
         segs[seg, pl.ds(PSI, N)] = ps[seg]
@@ -505,6 +532,12 @@
     zc[z] = leave_chips(None)[0]
     part = zc.at[z]
     group = [wires.go(part, part, tm_0=lax.rem(z + step, nz)) for step in range(1, nz)]
+    xv = chip_x[0]
+    for i in range(1, nx):
+        xv = jnp.where(x == i, chip_x[i], xv)
+    xv, c_plan = descend_x(xv, ctree, c)
+    xv, y_plan = descend_x(xv, ytree, y)
+    s_plan = final_x(xv, stree, hi_ref, lo_ref, s_all)
     from_slabs(zps, *z_behind, False)
     for copy in group:
         copy.wait_recv()
@@ -517,11 +550,10 @@
         leaving = jnp.where(z == i - 1, state, leaving)
 
     chip_u = leave_chips(leaving)
-    xv, uv = chip_x[0], chip_u[1]
+    uv = chip_u[1]
     for i in range(1, nx):
-        xv, uv = jnp.where(x == i, chip_x[i], xv), jnp.where(x == i, chip_u[i + 1], uv)
-    xv, uv = descend(xv, uv, ctree, c)
-    xv, uv = descend(xv, uv, ytree, y)
+        uv = jnp.where(x == i, chip_u[i + 1], uv)
+    uv = descend_u(descend_u(uv, c_plan), y_plan)
 
     homes, detours = [], []
 
@@ -535,7 +567,7 @@
         for there in (right, left) if first < half else others:
             homes.append(wires.go(out_buf.at[there, rows], target(first, count), track=there))
 
-    final_pass(xv, uv, stree, hi_ref, lo_ref, s_all, out_buf, sent)
+    final_u(uv, s_plan, hi_ref, lo_ref, s_all, out_buf, sent)
     out_ref[own_rows] = out_buf[y]
     for copy, rows, first, count in detours:
         copy.wait_recv()

time: 77.4 us -> 75.8 us (0.979)
  Pallas kernels: 74.6 us -> 73.6 us
    pallas_call x1, Pallas kernels: 74.6 us -> 73.6 us  [main_call(): pl.pallas_call(functools.partial(main_kernel, sizes), out_shape=jax.Shape...]
where the time goes in v2:
time: 75.8 us; the launch traced here: 75.3 us
  Pallas kernels  73.6 us (97%)
  local copies, waits for them, and re-layouts  1.67 us (2%)
    pallas_call x1, Pallas kernels, main_call(): pl.pallas_call(functools.partial(main_kernel, sizes), out_shape=jax.Shape...  73.6 us
    unnamed x1, local copies, waits for them, and re-layouts  1.67 us

profile of v2, /device:TPU:40, one launch (start us, length us, event | category | flops | bytes accessed | tf_op | source)
XLA Modules:
  0.0 75.3 jit_solution(17169890899529075315)
XLA Ops:
  0.0 73.6 %smooth.1 = f32[512,128]{1,0:T(8,128)} custom-call(s32[32]{0:T(128)} %refs_0_.1, bf16[64,128,128]{2,1,0:T(8,128)(2,1)} %refs_1_.1, bf16[64,128,128]{2,1,0:T(8,128)(2,1)} %refs_2_.1, bf16[64,128]{1,0:T(8,128)(2,1)} %refs_3_.1, f32[512,128]{1,0:T(8,128)} %bitcast.3), custom_call_target="tpu_custom_call" | custom-call | tf_op jit(solution)/shard_map/smooth/pallas_call | solution.py:590
  73.6 1.7 %copy.7 = f32[128,4,128]{2,1,0:T(4,128)} copy(f32[128,4,128]{2,1,0:T(4,128)} %bitcast.2) | data formatting | bytes 524288

commit v3 on v2

--- a/solution.py
+++ b/solution.py
@@ -446,21 +446,24 @@
         parts = [xbuf.at[lax.rem(x + step, nx), rows] for step in range(1, nx)] if nc > 1 else []
         return [wires.go(part, part, tm_2=1 - c) for part in parts]
 
+    far_first = sorted(range(1, nz), key=lambda step: -min(step, nz - step))
+
     def to_slabs(buf, rows, later):
         mine = pl.ds(pl.multiple_of(c * (rows // nc), 8), rows // nc)
         part = buf.at[z, mine]
-        moves = []
-        for step in range(1, nz):
+        moves = {}
+        for step in far_first:
             there = z + step if later else z - step
             copy = wires.make(part, part, tm_0=jnp.clip(there, 0, nz - 1))
             use = there < nz if later else jnp.logical_and(there >= 0, z < nz - 1)
-            moves.append((copy, use))
+            moves[step] = (copy, use)
             pl.when(use)(copy.start)
         return mine, moves
 
     def from_slabs(buf, mine, moves, later):
         shared = []
-        for step, (copy, _) in enumerate(moves, 1):
+        for step in far_first[::-1]:
+            copy = moves[step][0]
             source = z - step if later else z + step
             use = source >= 0 if later else source < nz - 1
             pl.when(use)(copy.wait_recv)
@@ -471,7 +474,7 @@
                 shared.append((over, use))
         for copy, use in shared:
             pl.when(use)(copy.wait_recv)
-        for copy, use in moves + shared:
+        for copy, use in list(moves.values()) + shared:
             pl.when(use)(copy.wait_send)
 
     y_ahead.finish()
@@ -485,28 +488,22 @@
     y_behind.relay()
     x_ahead.relay()
     y_behind.finish()
+    x_ahead.finish()
+    shared = share_start(own_a, share_a)
     fill(ytree, compose_behind)
     cbuf[c, pl.ds(W_MAT, ROWS + N)] = ytree[-1][0][pl.ds(W_MAT, ROWS + N)]
     c_behind.start()
-    x_ahead.finish()
-    shared = share_start(own_a, share_a)
-    c_behind.finish()
-    fill(ctree, compose_behind)
-    xbuf[x, pl.ds(W_MAT, ROWS + N)] = ctree[-1][0][pl.ds(W_MAT, ROWS + N)]
-    x_behind.start()
     for copy in shared:
         copy.wait_recv()
     fill(xtree, compose_ahead)
     total = xtree[-1][0]
     zpv[z] = total[pl.ds(0, ROWS)]
     z_ahead = to_slabs(zpv, ROWS, True)
+    c_behind.finish()
+    fill(ctree, compose_behind)
+    xbuf[x, pl.ds(W_MAT, ROWS + N)] = ctree[-1][0][pl.ds(W_MAT, ROWS + N)]
+    x_behind.start()
     x_behind.relay()
-    x_behind.finish()
-    for copy in share_start(own_b, share_b):
-        copy.wait_recv()
-    fill(xtree, compose_psi)
-    zps[z] = total[pl.ds(PSI, N)]
-    z_behind = to_slabs(zps, N, False)
     from_slabs(zpv, *z_ahead, True)
 
     zero = jnp.zeros((TR, N), F32)
@@ -521,6 +518,12 @@
     chip_x = [entering]
     for i in range(nx - 1):
         chip_x.append(middle_x(chip_x[-1], xbuf.at[i]))
+    x_behind.finish()
+    for copy in share_start(own_b, share_b):
+        copy.wait_recv()
+    fill(xtree, compose_psi)
+    zps[z] = total[pl.ds(PSI, N)]
+    z_behind = to_slabs(zps, N, False)
     chip_w = [product(chip_x[i], xbuf[i, pl.ds(W_MAT, N)]) + xbuf[i, pl.ds(W_ROW, TR)] for i in range(nx)]
 
     def leave_chips(state):
@@ -531,7 +534,7 @@
 
     zc[z] = leave_chips(None)[0]
     part = zc.at[z]
-    group = [wires.go(part, part, tm_0=lax.rem(z + step, nz)) for step in range(1, nz)]
+    group = [wires.go(part, part, tm_0=lax.rem(z + step, nz)) for step in far_first]
     xv = chip_x[0]
     for i in range(1, nx):
         xv = jnp.where(x == i, chip_x[i], xv)

time: 75.8 us -> 80.7 us (1.065)
  Pallas kernels: 73.6 us -> 78.3 us
    pallas_call x1, Pallas kernels: 73.6 us -> 78.3 us  [main_call(): pl.pallas_call(functools.partial(main_kernel, sizes), out_shape=jax.Shape...]
where the time goes in v3:
time: 80.7 us; the launch traced here: 79.9 us
  Pallas kernels  78.3 us (97%)
  local copies, waits for them, and re-layouts  1.67 us (2%)
    pallas_call x1, Pallas kernels, main_call(): pl.pallas_call(functools.partial(main_kernel, sizes), out_shape=jax.Shape...  78.3 us
    unnamed x1, local copies, waits for them, and re-layouts  1.67 us

profile of v3, /device:TPU:40, one launch (start us, length us, event | category | flops | bytes accessed | tf_op | source)
XLA Modules:
  0.0 79.9 jit_solution(5180884083809868802)
XLA Ops:
  0.0 78.3 %smooth.1 = f32[512,128]{1,0:T(8,128)} custom-call(s32[32]{0:T(128)} %refs_0_.1, bf16[64,128,128]{2,1,0:T(8,128)(2,1)} %refs_1_.1, bf16[64,128,128]{2,1,0:T(8,128)(2,1)} %refs_2_.1, bf16[64,128]{1,0:T(8,128)(2,1)} %refs_3_.1, f32[512,128]{1,0:T(8,128)} %bitcast.3), custom_call_target="tpu_custom_call" | custom-call | tf_op jit(solution)/shard_map/smooth/pallas_call | solution.py:593
  78.3 1.7 %copy.7 = f32[128,4,128]{2,1,0:T(4,128)} copy(f32[128,4,128]{2,1,0:T(4,128)} %bitcast.2) | data formatting | bytes 524288

commit v4 on v2

--- a/solution.py
+++ b/solution.py
@@ -446,21 +446,24 @@
         parts = [xbuf.at[lax.rem(x + step, nx), rows] for step in range(1, nx)] if nc > 1 else []
         return [wires.go(part, part, tm_2=1 - c) for part in parts]
 
+    far_first = sorted(range(1, nz), key=lambda step: -min(step, nz - step))
+
     def to_slabs(buf, rows, later):
         mine = pl.ds(pl.multiple_of(c * (rows // nc), 8), rows // nc)
         part = buf.at[z, mine]
-        moves = []
-        for step in range(1, nz):
+        moves = {}
+        for step in far_first:
             there = z + step if later else z - step
             copy = wires.make(part, part, tm_0=jnp.clip(there, 0, nz - 1))
             use = there < nz if later else jnp.logical_and(there >= 0, z < nz - 1)
-            moves.append((copy, use))
+            moves[step] = (copy, use)
             pl.when(use)(copy.start)
         return mine, moves
 
     def from_slabs(buf, mine, moves, later):
         shared = []
-        for step, (copy, _) in enumerate(moves, 1):
+        for step in far_first[::-1]:
+            copy = moves[step][0]
             source = z - step if later else z + step
             use = source >= 0 if later else source < nz - 1
             pl.when(use)(copy.wait_recv)
@@ -471,7 +474,7 @@
                 shared.append((over, use))
         for copy, use in shared:
             pl.when(use)(copy.wait_recv)
-        for copy, use in moves + shared:
+        for copy, use in list(moves.values()) + shared:
             pl.when(use)(copy.wait_send)
 
     y_ahead.finish()
@@ -531,7 +534,7 @@
 
     zc[z] = leave_chips(None)[0]
     part = zc.at[z]
-    group = [wires.go(part, part, tm_0=lax.rem(z + step, nz)) for step in range(1, nz)]
+    group = [wires.go(part, part, tm_0=lax.rem(z + step, nz)) for step in far_first]
     xv = chip_x[0]
     for i in range(1, nx):
         xv = jnp.where(x == i, chip_x[i], xv)
@@ -631,7 +634,7 @@
             pltpu.SemaphoreType.DMA((links,)),
         ],
         compiler_params=pltpu.CompilerParams(
-            collective_id=1, has_side_effects=True, vmem_limit_bytes=67043328
+            collective_id=1, has_side_effects=True, vmem_limit_bytes=56250000
         ),
         name="smooth",
     )(ids, dyn, smooth, gain, obs)

time: 75.8 us -> 75.1 us (level)
  Pallas kernels: 73.6 us -> 71.8 us
    pallas_call x1, Pallas kernels: 73.6 us -> 71.8 us  [main_call(): pl.pallas_call(functools.partial(main_kernel, sizes), out_shape=jax.Shape...]
    unnamed x1 -> x5, local copies, waits for them, and re-layouts: 1.67 us -> 2.08 us
where the time goes in v4:
time: 75.1 us; the launch traced here: 73.9 us
  Pallas kernels  71.8 us (96%)
  local copies, waits for them, and re-layouts  2.08 us (3%)
    pallas_call x1, Pallas kernels, main_call(): pl.pallas_call(functools.partial(main_kernel, sizes), out_shape=jax.Shape...  71.8 us
    unnamed x5, local copies, waits for them, and re-layouts  2.08 us

profile of v4, /device:TPU:40, one launch (start us, length us, event | category | flops | bytes accessed | tf_op | source)
XLA Modules:
  0.0 73.9 jit_solution(11958047255293698385)
XLA Ops:
  0.0 0.0 copy-start
  0.0 0.7 copy-done
  0.7 0.0 copy-start.1
  0.7 0.7 copy-done.1
  1.4 71.8 %smooth.1 = f32[512,128]{1,0:T(8,128)S(1)} custom-call(s32[32]{0:T(128)S(1)} %copy-done.1, bf16[64,128,128]{2,1,0:T(8,128)(2,1)} %refs_1_.1, bf16[64,128,128]{2,1,0:T(8,128)(2,1)} %refs_2_.1, bf16[64,128]{1,0:T(8,128)(2,1)S(1)} %copy-done, f32[512,128]{1,0:T(8,128)} %bitcast.3), custom_call_target="tpu_custom_call" | custom-call | tf_op jit(solution)/shard_map/smooth/pallas_call | solution.py:593
  73.2 0.7 copy.7
Async XLA Ops:
  0.0 0.7 copy-start
  0.7 0.7 copy-start.1
